TPU v7x, 32 devices: a whole 2x2x4 slice. The times are simulated.
32 devices in a mesh: mem: 4 (over x, core), lat: 8 (over z, y).
Axes of the slice: x: 2, y: 2, z: 4, core: 2. Of those that a mesh axis runs over, the one named last changes fastest.
Arguments:
- perturbation: bfloat16 [64, 128, 2048], P('mem', 'lat'), may hold values from -6 to 6
- obs_cells: int32 [8, 2048], P('lat'), may hold values from 0 to 32767
- obs_count: int32 [8], P('lat'), may hold values from 682 to 2048, as said below
- innovation: float32 [8, 2048], P('lat'), may hold values from -8 to 8
- obs_scale: float32 [8, 2048], P('lat'), may hold values from 0.3 to 3
Outputs:
- control: float32 [64, 64, 1024], P('mem', 'lat')
- increment: float32 [128, 2048], P('lat', 'mem')
Inputs may be any that keep to these rules, and one draw needn't show every extreme that they name: `obs_count`: at most 2048 live slots in a band, and some band has exactly 2048.
All inputs are finite; a program needn't handle non-finite values.
Results may differ from a plain program's by a relative error of at most 0.00035.
Values sent between devices are 32-bit elements; how exact they have to be, the bound alone decides.
No kernel may reach another device: no remote copies, remote signals or barrier semaphores. Data moves between devices by JAX's collectives and lax.ppermute only.
A program may use at most 64 MiB of HBM per device.

v0:
```python
import jax
import jax.numpy as jnp
from jax import lax
from jax.sharding import PartitionSpec as P

HALO = 8
LSIG = 3
ITERS = 3


def padded_2(block, sides, width):
    for axis, dim in sides:
        count = lax.axis_size(axis)
        forward = [(i, i + 1) for i in range(count - 1)]
        backward = [(target, source) for source, target in forward]
        low = lax.ppermute(
            lax.slice_in_dim(block, block.shape[dim] - width, None, axis=dim), axis, forward
        )
        high = lax.ppermute(lax.slice_in_dim(block, 0, width, axis=dim), axis, backward)
        block = jnp.concatenate([low, block, high], axis=dim)
    return block


def lat_weights():
    offsets = jnp.arange(2 * HALO + 1).astype(jnp.float32) - HALO
    spread = HALO / 2.0
    return 0.5 * jnp.exp(-offsets * offsets / (2.0 * spread * spread))


def lon_weights(coarse_cols):
    columns = jnp.arange(coarse_cols)
    distance = jnp.abs(columns[:, None] - columns[None, :])
    distance = jnp.minimum(distance, coarse_cols - distance).astype(jnp.float32)
    return jnp.exp(-distance * distance / (2.0 * LSIG * LSIG))


def band_matrix(row_count, lat_taps):
    rows = jnp.arange(row_count)[:, None]
    columns = jnp.arange(row_count + 2 * HALO)[None, :]
    offset_grid = columns - rows
    matrix = jnp.zeros((row_count, row_count + 2 * HALO), jnp.float32)
    for offset in range(2 * HALO + 1):
        matrix = matrix + jnp.where(offset_grid == offset, lat_taps[offset], 0.0)
    return matrix


def widen_lon(coarse):
    odd_part = 0.5 * (coarse + jnp.roll(coarse, -1, axis=-1))
    return jnp.stack([coarse, odd_part], axis=-1).reshape(
        coarse.shape[:-1] + (2 * coarse.shape[-1],)
    )


def narrow_lon(fine):
    paired = fine.reshape(fine.shape[:-1] + (fine.shape[-1] // 2, 2))
    odd_part = paired[..., 1]
    return paired[..., 0] + 0.5 * odd_part + 0.5 * jnp.roll(odd_part, 1, axis=-1)


def on_device(perturbation, obs_cells, obs_count, innovation, obs_scale):
    mem_count = lax.axis_size("mem")
    local_members, fine_rows, lon_cells = perturbation.shape
    coarse_rows = fine_rows // 2
    coarse_cols = lon_cells // 2
    member_scale = (local_members * mem_count - 1) ** (-0.5)
    lat_taps = lat_weights()
    banded = band_matrix(coarse_rows, lat_taps)
    circulant = lon_weights(coarse_cols)
    obs_index = obs_cells[0]
    row_index = obs_index // lon_cells
    col_index = obs_index % lon_cells
    active = jnp.arange(obs_index.shape[0]) < obs_count[0]
    is_first = lax.axis_index("mem") == 0
    target = innovation[0]
    saturation = obs_scale[0]

    def smooth(coarse):
        padded = padded_2(coarse, (("lat", 1),), HALO)
        return jnp.einsum(
            "ij,mjk->mik",
            banded,
            padded,
            precision=lax.Precision.HIGHEST,
            preferred_element_type=jnp.float32,
        )

    bend_mask = active & is_first
    increment = jnp.zeros((fine_rows, lon_cells), jnp.float32)
    control = jnp.zeros((local_members, coarse_rows, coarse_cols), jnp.float32)
    observed = jnp.zeros(obs_index.shape, jnp.float32)
    for iteration in range(ITERS):
        misfit = target - observed
        bounded = jnp.tanh(misfit / saturation)
        pull = jnp.where(active, saturation * bounded, 0.0)
        weight = jnp.where(bend_mask, 1.0 - bounded * bounded, 0.0)
        obs_field = (
            jnp.zeros((fine_rows * lon_cells,), jnp.float32)
            .at[obs_index]
            .add(pull)
            .reshape(fine_rows, lon_cells)
        )
        weighted = perturbation.astype(jnp.float32) * obs_field[None] * member_scale
        folded = narrow_lon(weighted.reshape(local_members, coarse_rows, 2, lon_cells).sum(axis=2))
        gradient = control - smooth(
            jnp.dot(
                folded,
                circulant,
                precision=lax.Precision.HIGHEST,
                preferred_element_type=jnp.float32,
            )
        )
        local_norm = jnp.sum(gradient * gradient)
        grad_norm = lax.psum(local_norm, ("mem", "lat"))
        direction = -gradient
        smoothed = smooth(direction)
        along = jnp.dot(
            smoothed, circulant, precision=lax.Precision.HIGHEST, preferred_element_type=jnp.float32
        )
        fine_block = jnp.repeat(widen_lon(along), 2, axis=1)
        partial_image = (
            jnp.sum(perturbation.astype(jnp.float32) * fine_block, axis=0) * member_scale
        )
        hits = lax.psum(partial_image[row_index, col_index], "mem")
        local_bend = jnp.sum(weight * hits * hits)
        bending = lax.psum(local_bend, ("mem", "lat"))
        step_size = grad_norm / (grad_norm + bending + 1e-06)
        control = control + step_size * direction
        increment = increment + step_size * partial_image
        observed = observed + step_size * hits
    increment = lax.psum_scatter(increment, "mem", scatter_dimension=1, tiled=True)
    return (control, increment)


def solution(mesh):
    in_specs = (P("mem", "lat", None), P("lat", None), P("lat"), P("lat", None), P("lat", None))
    out_specs = (P("mem", "lat", None), P("lat", "mem"))
    return jax.shard_map(
        on_device, mesh=mesh, in_specs=in_specs, out_specs=out_specs, check_vma=False
    )
```

profile of v0, /device:TPU:0, one launch (start us, length us, event | category | flops | bytes accessed | tf_op | source)
XLA Modules:
  0.0 612.5 jit_solution(4146181760270412733)
XLA Ops:
  9.4 11.3 %scatter_custom_fusion = f32[32768]{0:T(1024)S(1)} fusion(s32[2048]{0:T(1024)S(1)} %bitcast.168, f32[2048]{0:T(1024)S(1)} %multiply_select_fusion.2, f32[]{:T(128)} %constant.31.clone.1), kind=kCustom, calls=%fused_computation.133 | custom fusion | flops 2048 | bytes 131076 | tf_op jit(solution)/shard_map/scatter-add | solution.py:99
  24.5 4.3 reduce_sum.108
  28.8 4.8 copy.19
  33.6 7.2 %fusion.188 = (f32[16,8,1024,1]{0,1,3,2:T(8,128)}, f32[16,8,1024,1]{0,1,3,2:T(8,128)}) fusion(f32[16,8,1024,2]{0,1,3,2:T(8,128)} %bitcast.146), kind=kLoop, calls=%fused_computation.221 | loop fusion | bytes 2097152 | tf_op jit(solution)/shard_map/slice | solution.py:57
  46.9 4.0 fusion.14
  50.9 4.9 collective-permute-start
  58.1 10.6 %select_add_fusion = f32[8,24]{1,0:T(8,128)S(1)} fusion(f32[]{:T(128)} %bitcast.25, f32[]{:T(128)} %bitcast.24, f32[]{:T(128)} %bitcast.23, f32[]{:T(128)} %bitcast.22, f32[]{:T(128)} %bitcast.21, f32[]{:T(128)} %bitcast.20, f32[]{:T(128)} %bitcast.19, f32[]{:T(128)} %bitcast.18, f32[]{:T(128)} %bitcast.17, f32[]{:T(128)} %bitcast.16, f32[]{:T(128)} %bitcast.15, ...), kind=kLoop, calls=%fused_computation.169 | loop fusion | flops 9792 | bytes 836 | tf_op jit(solution)/shard_map/add | solution.py:43
  68.7 9.5 %collective-permute-done = f32[16,8,1024]{2,1,0:T(8,128)S(1)} collective-permute-done((f32[16,8,1024]{2,1,0:T(8,128)S(1)}, f32[16,8,1024]{2,1,0:T(8,128)S(1)}, u32[]{:S(2)}, u32[]{:S(2)}) %collective-permute-start) | collective-permute-done | bytes 524320 | tf_op jit(solution)/shard_map/ppermute | solution.py:16
  79.9 4.4 collective-permute-start.2
  85.6 20.2 %collective-permute-done.2 = f32[16,8,1024]{2,1,0:T(8,128)S(1)} collective-permute-done((f32[16,8,1024]{2,1,0:T(8,128)S(1)}, f32[16,8,1024]{2,1,0:T(8,128)S(1)}, u32[]{:S(2)}, u32[]{:S(2)}) %collective-permute-start.2) | collective-permute-done | bytes 524320 | tf_op jit(solution)/shard_map/ppermute | solution.py:16
  106.7 3.9 fusion.12
  111.1 6.2 %copy.22 = f32[16,8,1024,2]{0,1,3,2:T(8,128)} copy(f32[16,8,1024,2]{2,1,0,3:T(8,128)S(1)} %pad_maximum_fusion) | data formatting | bytes 2097152 | tf_op jit(solution)/shard_map/stack | solution.py:49
  117.3 5.4 copy.23
  125.2 3.7 reshape.188
  130.8 16.6 %gather_fusion = f32[2048]{0:T(1024)S(1)} fusion(f32[16,2048]{1,0:T(8,128)S(1)} %broadcast_multiply_fusion.2, s32[2048]{0:T(1024)S(1)} %bitcast.140), kind=kCustom, calls=%fused_computation | custom fusion | bytes 32768 | tf_op jit(solution)/shard_map/gather | solution.py:123
  147.4 5.8 psum.64
  153.8 45.1 %all-reduce.2 = (f32[]{:T(128)}, f32[]{:T(128)}) all-reduce(f32[]{:T(128)} %get-tuple-element.20, f32[]{:T(128)} %fusion.124), channel_id=1, replica_groups=mesh['mem'=4,'lat'=8] {'mem','lat'}, use_global_device_ids=true, to_apply=%region_3.4 | all-reduce | flops 2 | bytes 16 | tf_op jit(solution)/shard_map/psum | solution.py:113
  200.9 11.3 %scatter_custom_fusion.1 = f32[32768]{0:T(1024)S(1)} fusion(s32[2048]{0:T(1024)S(1)} %bitcast.169, f32[2048]{0:T(1024)S(1)} %multiply_select_fusion.1, f32[]{:T(128)} %constant.31.clone.1), kind=kCustom, calls=%fused_computation.131 | custom fusion | flops 2048 | bytes 131076 | tf_op jit(solution)/shard_map/scatter-add | solution.py:99
  217.3 4.3 reduce_sum.112
  221.6 4.8 copy.24
  226.4 7.2 %fusion.187 = (f32[16,8,1024,1]{0,1,3,2:T(8,128)}, f32[16,8,1024,1]{0,1,3,2:T(8,128)}) fusion(f32[16,8,1024,2]{0,1,3,2:T(8,128)} %bitcast.147), kind=kLoop, calls=%fused_computation.220 | loop fusion | bytes 2097152 | tf_op jit(solution)/shard_map/slice | solution.py:57
  239.7 4.0 fusion.10
  243.7 4.5 collective-permute-start.4
  249.7 19.2 %collective-permute-done.4 = f32[16,8,1024]{2,1,0:T(8,128)S(1)} collective-permute-done((f32[16,8,1024]{2,1,0:T(8,128)S(1)}, f32[16,8,1024]{2,1,0:T(8,128)S(1)}, u32[]{:S(2)}, u32[]{:S(2)}) %collective-permute-start.4) | collective-permute-done | bytes 524320 | tf_op jit(solution)/shard_map/ppermute | solution.py:16
  270.4 4.4 collective-permute-start.6
  276.1 18.5 %collective-permute-done.6 = f32[16,8,1024]{2,1,0:T(8,128)S(1)} collective-permute-done((f32[16,8,1024]{2,1,0:T(8,128)S(1)}, f32[16,8,1024]{2,1,0:T(8,128)S(1)}, u32[]{:S(2)}, u32[]{:S(2)}) %collective-permute-start.6) | collective-permute-done | bytes 524320 | tf_op jit(solution)/shard_map/ppermute | solution.py:16
  295.5 3.9 fusion.8
  299.9 6.2 %copy.27 = f32[16,8,1024,2]{0,1,3,2:T(8,128)} copy(f32[16,8,1024,2]{2,1,0,3:T(8,128)S(1)} %pad_maximum_fusion.1) | data formatting | bytes 2097152 | tf_op jit(solution)/shard_map/stack | solution.py:49
  306.1 5.4 copy.28
  319.6 16.6 %gather_fusion.1 = f32[2048]{0:T(1024)S(1)} fusion(f32[16,2048]{1,0:T(8,128)S(1)} %broadcast_multiply_fusion.1, s32[2048]{0:T(1024)S(1)} %bitcast.141), kind=kCustom, calls=%fused_computation.1 | custom fusion | bytes 32768 | tf_op jit(solution)/shard_map/gather | solution.py:123
  336.2 6.1 psum.67
  342.9 46.1 %all-reduce.1 = (f32[]{:T(128)}, f32[]{:T(128)}) all-reduce(f32[]{:T(128)} %get-tuple-element.18, f32[]{:T(128)} %fusion.125), channel_id=1, replica_groups=mesh['mem'=4,'lat'=8] {'mem','lat'}, use_global_device_ids=true, to_apply=%region_11.12 | all-reduce | flops 2 | bytes 16 | tf_op jit(solution)/shard_map/psum | solution.py:113
  391.7 11.4 %scatter_custom_fusion.2 = f32[32768]{0:T(1024)S(1)} fusion(s32[2048]{0:T(1024)} %bitcast.170, f32[2048]{0:T(1024)S(1)} %get-tuple-element.8, f32[]{:T(128)} %constant.31.clone.1), kind=kCustom, calls=%fused_computation.129 | custom fusion | flops 2048 | bytes 131584 | tf_op jit(solution)/shard_map/scatter-add | solution.py:99
  408.2 4.3 reduce_sum.116
  412.5 4.8 copy.29
  417.3 7.2 %fusion.186 = (f32[16,8,1024,1]{0,1,3,2:T(8,128)}, f32[16,8,1024,1]{0,1,3,2:T(8,128)}) fusion(f32[16,8,1024,2]{0,1,3,2:T(8,128)} %bitcast.148), kind=kLoop, calls=%fused_computation.219 | loop fusion | bytes 2097152 | tf_op jit(solution)/shard_map/slice | solution.py:57
  431.2 5.1 fusion.6
  436.3 4.5 collective-permute-start.8
  442.3 19.2 %collective-permute-done.8 = f32[16,8,1024]{2,1,0:T(8,128)S(1)} collective-permute-done((f32[16,8,1024]{2,1,0:T(8,128)S(1)}, f32[16,8,1024]{2,1,0:T(8,128)S(1)}, u32[]{:S(2)}, u32[]{:S(2)}) %collective-permute-start.8) | collective-permute-done | bytes 524320 | tf_op jit(solution)/shard_map/ppermute | solution.py:16
  463.9 4.4 collective-permute-start.10
  469.6 18.6 %collective-permute-done.10 = f32[16,8,1024]{2,1,0:T(8,128)S(1)} collective-permute-done((f32[16,8,1024]{2,1,0:T(8,128)S(1)}, f32[16,8,1024]{2,1,0:T(8,128)S(1)}, u32[]{:S(2)}, u32[]{:S(2)}) %collective-permute-start.10) | collective-permute-done | bytes 524320 | tf_op jit(solution)/shard_map/ppermute | solution.py:16
  490.3 3.9 fusion.4
  494.7 6.2 %copy.32 = f32[16,8,1024,2]{0,1,3,2:T(8,128)} copy(f32[16,8,1024,2]{2,1,0,3:T(8,128)S(1)} %pad_maximum_fusion.2) | data formatting | bytes 2097152 | tf_op jit(solution)/shard_map/stack | solution.py:49
  500.9 5.4 copy.33
  514.4 16.6 %gather_fusion.2 = f32[2048]{0:T(1024)S(1)} fusion(f32[16,2048]{1,0:T(8,128)S(1)} %broadcast_multiply_fusion, s32[2048]{0:T(1024)S(1)} %bitcast.142), kind=kCustom, calls=%fused_computation.2 | custom fusion | bytes 32768 | tf_op jit(solution)/shard_map/gather | solution.py:123
  531.0 5.8 psum.70
  537.5 45.1 %all-reduce = (f32[]{:T(128)}, f32[]{:T(128)}) all-reduce(f32[]{:T(128)} %get-tuple-element.17, f32[]{:T(128)} %fusion.126), channel_id=1, replica_groups=mesh['mem'=4,'lat'=8] {'mem','lat'}, use_global_device_ids=true, to_apply=%region_19.20 | all-reduce | flops 2 | bytes 16 | tf_op jit(solution)/shard_map/psum | solution.py:113
  586.2 19.0 %reduce-scatter.2.cloned.1.call-done = f32[16,512]{1,0:T(8,128)} async-done(((f32[16,2048]{1,0:T(8,128)}), f32[16,512]{1,0:T(8,128)}) %reduce-scatter.2.cloned.1.call-update) | async-done | bytes 32784 | tf_op jit(solution)/shard_map/reduce_scatter | solution.py:130
  (95 shorter events, 78.9 us)
Async XLA Ops:
  7.2 598.1 %reduce-scatter.2.cloned.1.call-start = ((), (), s32[]{:S(2)}) async-start(), calls=%async_computation.1 | async-start | bytes 163840 | tf_op jit(solution)/shard_map/reduce_scatter | solution.py:130
  8.7 192.2 %copy-start.10 = (s32[2048,1]{0,1:T(1,128)}, s32[2048,1]{0,1:T(1,128)S(1)}, u32[]{:S(2)}) copy-start(s32[2048,1]{0,1:T(1,128)S(1)} %get-tuple-element.23) | copy-start | bytes 24580
  50.9 27.3 %collective-permute-start = (f32[16,8,1024]{2,1,0:T(8,128)S(1)}, f32[16,8,1024]{2,1,0:T(8,128)S(1)}, u32[]{:S(2)}, u32[]{:S(2)}) collective-permute-start(f32[16,8,1024]{2,1,0:T(8,128)S(1)} %fusion.14), channel_id=1, source_target_pairs={{0,1},{1,2},{2,3},{3,4},{4,5},{5,6},{6,7},{8,9},{9,10},{10,11},{11... | collective-permute-start | bytes 1572872 | tf_op jit(solution)/shard_map/ppermute | solution.py:16
  55.8 22.4 %collective-permute-start.1 = (f32[16,8,1024]{2,1,0:T(8,128)S(1)}, f32[16,8,1024]{2,1,0:T(8,128)S(1)}, u32[]{:S(2)}, u32[]{:S(2)}) collective-permute-start(f32[16,8,1024]{2,1,0:T(8,128)S(1)} %fusion.14), channel_id=1, source_target_pairs={{1,0},{2,1},{3,2},{4,3},{5,4},{6,5},{7,6},{9,8},{10,9},{11,10},{12... | collective-permute-start | bytes 1572872 | tf_op jit(solution)/shard_map/ppermute | solution.py:19
  68.7 225.9 %copy-start.7 = (f32[8,24]{1,0:T(8,128)}, f32[8,24]{1,0:T(8,128)S(1)}, u32[]{:S(2)}) copy-start(f32[8,24]{1,0:T(8,128)S(1)} %select_add_fusion) | copy-start | bytes 2308
  79.9 25.9 %collective-permute-start.2 = (f32[16,8,1024]{2,1,0:T(8,128)S(1)}, f32[16,8,1024]{2,1,0:T(8,128)S(1)}, u32[]{:S(2)}, u32[]{:S(2)}) collective-permute-start(f32[16,8,1024]{2,1,0:T(8,128)S(1)} %get-tuple-element.21), channel_id=1, source_target_pairs={{0,1},{1,2},{2,3},{3,4},{4,5},{5,6},{6,7},{8,9},{9,10},{10,11},{11... | collective-permute-start | bytes 1572872 | tf_op jit(solution)/shard_map/ppermute | solution.py:16
  84.3 21.5 %collective-permute-start.3 = (f32[16,8,1024]{2,1,0:T(8,128)S(1)}, f32[16,8,1024]{2,1,0:T(8,128)S(1)}, u32[]{:S(2)}, u32[]{:S(2)}) collective-permute-start(f32[16,8,1024]{2,1,0:T(8,128)S(1)} %get-tuple-element.21), channel_id=1, source_target_pairs={{1,0},{2,1},{3,2},{4,3},{5,4},{6,5},{7,6},{9,8},{10,9},{11,10},{12... | collective-permute-start | bytes 1572872 | tf_op jit(solution)/shard_map/ppermute | solution.py:19
  122.7 6.2 %copy-start = (bf16[16,16,2048]{2,1,0:T(8,128)(2,1)S(1)}, bf16[16,16,2048]{2,1,0:T(8,128)(2,1)}, u32[]{:S(2)}) copy-start(bf16[16,16,2048]{2,1,0:T(8,128)(2,1)} %param.5) | copy-start | bytes 3145732
  130.7 22.5 %copy-start.2 = (f32[1,2048]{1,0:T(1,128)S(1)}, f32[1,2048]{1,0:T(1,128)}, u32[]{:S(2)}) copy-start(f32[1,2048]{1,0:T(1,128)} %param.9) | copy-start | bytes 24580
  130.8 22.5 %copy-start.3 = (f32[1,2048]{1,0:T(1,128)S(1)}, f32[1,2048]{1,0:T(1,128)}, u32[]{:S(2)}) copy-start(f32[1,2048]{1,0:T(1,128)} %param.8) | copy-start | bytes 24580
  153.2 68.4 %copy-start.5 = (f32[2048]{0:T(1024)}, f32[2048]{0:T(1024)S(1)}, u32[]{:S(2)}) copy-start(f32[2048]{0:T(1024)S(1)} %psum.64) | copy-start | bytes 24580
  243.7 25.1 %collective-permute-start.4 = (f32[16,8,1024]{2,1,0:T(8,128)S(1)}, f32[16,8,1024]{2,1,0:T(8,128)S(1)}, u32[]{:S(2)}, u32[]{:S(2)}) collective-permute-start(f32[16,8,1024]{2,1,0:T(8,128)S(1)} %fusion.10), channel_id=1, source_target_pairs={{0,1},{1,2},{2,3},{3,4},{4,5},{5,6},{6,7},{8,9},{9,10},{10,11},{11... | collective-permute-start | bytes 1572872 | tf_op jit(solution)/shard_map/ppermute | solution.py:16
  248.2 20.6 %collective-permute-start.5 = (f32[16,8,1024]{2,1,0:T(8,128)S(1)}, f32[16,8,1024]{2,1,0:T(8,128)S(1)}, u32[]{:S(2)}, u32[]{:S(2)}) collective-permute-start(f32[16,8,1024]{2,1,0:T(8,128)S(1)} %fusion.10), channel_id=1, source_target_pairs={{1,0},{2,1},{3,2},{4,3},{5,4},{6,5},{7,6},{9,8},{10,9},{11,10},{12... | collective-permute-start | bytes 1572872 | tf_op jit(solution)/shard_map/ppermute | solution.py:19
  270.4 24.2 %collective-permute-start.6 = (f32[16,8,1024]{2,1,0:T(8,128)S(1)}, f32[16,8,1024]{2,1,0:T(8,128)S(1)}, u32[]{:S(2)}, u32[]{:S(2)}) collective-permute-start(f32[16,8,1024]{2,1,0:T(8,128)S(1)} %get-tuple-element.19), channel_id=1, source_target_pairs={{0,1},{1,2},{2,3},{3,4},{4,5},{5,6},{6,7},{8,9},{9,10},{10,11},{11... | collective-permute-start | bytes 1572872 | tf_op jit(solution)/shard_map/ppermute | solution.py:16
  274.8 19.8 %collective-permute-start.7 = (f32[16,8,1024]{2,1,0:T(8,128)S(1)}, f32[16,8,1024]{2,1,0:T(8,128)S(1)}, u32[]{:S(2)}, u32[]{:S(2)}) collective-permute-start(f32[16,8,1024]{2,1,0:T(8,128)S(1)} %get-tuple-element.19), channel_id=1, source_target_pairs={{1,0},{2,1},{3,2},{4,3},{5,4},{6,5},{7,6},{9,8},{10,9},{11,10},{12... | collective-permute-start | bytes 1572872 | tf_op jit(solution)/shard_map/ppermute | solution.py:19
  319.6 22.7 %copy-start.4 = (f32[1,2048]{1,0:T(1,128)S(1)}, f32[1,2048]{1,0:T(1,128)}, u32[]{:S(2)}) copy-start(f32[1,2048]{1,0:T(1,128)} %param.8) | copy-start | bytes 24580
  319.6 22.7 %copy-start.6 = (f32[2048]{0:T(1024)S(1)}, f32[2048]{0:T(1024)}, u32[]{:S(2)}) copy-start(f32[2048]{0:T(1024)} %copy-done.5) | copy-start | bytes 24580
  431.2 30.3 %copy-start.8 = (f32[8,24]{1,0:T(8,128)S(1)}, f32[8,24]{1,0:T(8,128)}, u32[]{:S(2)}) copy-start(f32[8,24]{1,0:T(8,128)} %copy-done.7) | copy-start | bytes 2308
  436.3 25.3 %collective-permute-start.8 = (f32[16,8,1024]{2,1,0:T(8,128)S(1)}, f32[16,8,1024]{2,1,0:T(8,128)S(1)}, u32[]{:S(2)}, u32[]{:S(2)}) collective-permute-start(f32[16,8,1024]{2,1,0:T(8,128)S(1)} %fusion.6), channel_id=1, source_target_pairs={{0,1},{1,2},{2,3},{3,4},{4,5},{5,6},{6,7},{8,9},{9,10},{10,11},{11... | collective-permute-start | bytes 1572872 | tf_op jit(solution)/shard_map/ppermute | solution.py:16
  440.8 20.8 %collective-permute-start.9 = (f32[16,8,1024]{2,1,0:T(8,128)S(1)}, f32[16,8,1024]{2,1,0:T(8,128)S(1)}, u32[]{:S(2)}, u32[]{:S(2)}) collective-permute-start(f32[16,8,1024]{2,1,0:T(8,128)S(1)} %fusion.6), channel_id=1, source_target_pairs={{1,0},{2,1},{3,2},{4,3},{5,4},{6,5},{7,6},{9,8},{10,9},{11,10},{12... | collective-permute-start | bytes 1572872 | tf_op jit(solution)/shard_map/ppermute | solution.py:19
  463.9 24.3 %collective-permute-start.10 = (f32[16,8,1024]{2,1,0:T(8,128)S(1)}, f32[16,8,1024]{2,1,0:T(8,128)S(1)}, u32[]{:S(2)}, u32[]{:S(2)}) collective-permute-start(f32[16,8,1024]{2,1,0:T(8,128)S(1)} %get-tuple-element.16), channel_id=1, source_target_pairs={{0,1},{1,2},{2,3},{3,4},{4,5},{5,6},{6,7},{8,9},{9,10},{10,11},{11... | collective-permute-start | bytes 1572872 | tf_op jit(solution)/shard_map/ppermute | solution.py:16
  468.3 19.9 %collective-permute-start.11 = (f32[16,8,1024]{2,1,0:T(8,128)S(1)}, f32[16,8,1024]{2,1,0:T(8,128)}, u32[]{:S(2)}, u32[]{:S(2)}) collective-permute-start(f32[16,8,1024]{2,1,0:T(8,128)S(1)} %get-tuple-element.16), channel_id=1, source_target_pairs={{1,0},{2,1},{3,2},{4,3},{5,4},{6,5},{7,6},{9,8},{10,9},{11,10},{12... | collective-permute-start | bytes 1572872 | tf_op jit(solution)/shard_map/ppermute | solution.py:19
  514.4 22.5 %copy-start.9 = (f32[2048]{0:T(1024)S(1)}, f32[2048]{0:T(1024)}, u32[]{:S(2)}) copy-start(f32[2048]{0:T(1024)} %get-tuple-element.9) | copy-start | bytes 24580
  514.4 70.9 %copy-start.1 = (f32[16,8,1024]{2,1,0:T(8,128)S(1)}, f32[16,8,1024]{2,1,0:T(8,128)}, u32[]{:S(2)}) copy-start(f32[16,8,1024]{2,1,0:T(8,128)} %get-tuple-element.42) | copy-start | bytes 1572868
Sparse Core Ops, SparseCore 0:
  585.4 19.8 reduce-scatter.1
where the time goes:
time: 622 us; the launch traced here: 613 us
  local copies, waits for them, and re-layouts  169 us (27%)
  blocking collectives  154 us (25%)
  waiting for transfers between devices  124 us (20%)
  other arithmetic  74.9 us (12%)
  starting transfers between devices  35.5 us (6%)
  matrix products  33.7 us (5%)
  between operations  21.7 us (3%)
    psum x3, blocking collectives, on_device(): grad_norm = lax.psum(local_norm, ('mem', 'lat'))  136 us
    ppermute x6, waiting for transfers between devices, padded_2(): lax.ppermute(lax.slice_in_dim(block, block.shape[dim] - width, None, axis...  105 us
    gather x3, local copies, waits for them, and re-layouts, on_device(): hits = lax.psum(partial_image[row_index, col_index], 'mem')  50 us
    scatter-add x3, other arithmetic, on_device(): obs_field = jnp.zeros((fine_rows * lon_cells,), jnp.float32).at[obs_index...  34 us
    ppermute x6, starting transfers between devices, padded_2(): lax.ppermute(lax.slice_in_dim(block, block.shape[dim] - width, None, axis...  27.1 us
    slice x3, local copies, waits for them, and re-layouts, narrow_lon(): paired[..., 0] + 0.5 * odd_part + 0.5 * jnp.roll(odd_part, 1, axis=-1)  21.6 us
    reduce_scatter x1, waiting for transfers between devices, on_device(): lax.psum_scatter(increment, 'mem', scatter_dimension=1, tiled=True)  19 us
    another operation x3, local copies, waits for them, and re-layouts, widen_lon(): jnp.stack([coarse, odd_part], axis=-1)  18.6 us
  transfers between devices with their start and end apart: 13, of which 7 were waited for; matrix products, arithmetic and copies ran while one was open for 2% of the time, Pallas kernels for 0%

commit v1 on v0

--- a/solution.py
+++ b/solution.py
@@ -6,6 +6,11 @@
 HALO = 8
 LSIG = 3
 ITERS = 3
+
+
+def edges_manage(xs):
+    kept_arr = lax.all_gather(xs, "mem")
+    return jnp.sum(kept_arr, 0)
 
 
 def padded_2(block, sides, width):
@@ -120,7 +125,7 @@
         partial_image = (
             jnp.sum(perturbation.astype(jnp.float32) * fine_block, axis=0) * member_scale
         )
-        hits = lax.psum(partial_image[row_index, col_index], "mem")
+        hits = edges_manage(partial_image[row_index, col_index])
         local_bend = jnp.sum(weight * hits * hits)
         bending = lax.psum(local_bend, ("mem", "lat"))
         step_size = grad_norm / (grad_norm + bending + 1e-06)

time: 622 us -> 620 us (level)
  blocking collectives: 154 us -> 146 us
    psum x3 -> x0, blocking collectives: 17.6 us -> none  [on_device(): hits = lax.psum(partial_image[row_index, col_index], 'mem')]
    all_gather x0 -> x3, blocking collectives: none -> 15.6 us  [edges_manage(): kept_arr = lax.all_gather(xs, 'mem')]
where the time goes in v1:
time: 620 us; the launch traced here: 610 us
  local copies, waits for them, and re-layouts  169 us (27%)
  blocking collectives  146 us (24%)
  waiting for transfers between devices  129 us (21%)
  other arithmetic  74.9 us (12%)
  starting transfers between devices  35.5 us (6%)
  matrix products  33.7 us (5%)
  between operations  21.7 us (4%)
    psum x3, blocking collectives, on_device(): grad_norm = lax.psum(local_norm, ('mem', 'lat'))  131 us
    ppermute x6, waiting for transfers between devices, padded_2(): lax.ppermute(lax.slice_in_dim(block, block.shape[dim] - width, None, axis...  109 us
    gather x3, local copies, waits for them, and re-layouts, on_device(): hits = edges_manage(partial_image[row_index, col_index])  50 us
    scatter-add x3, other arithmetic, on_device(): obs_field = jnp.zeros((fine_rows * lon_cells,), jnp.float32).at[obs_index...  34 us
    ppermute x6, starting transfers between devices, padded_2(): lax.ppermute(lax.slice_in_dim(block, block.shape[dim] - width, None, axis...  27.1 us
    slice x3, local copies, waits for them, and re-layouts, narrow_lon(): paired[..., 0] + 0.5 * odd_part + 0.5 * jnp.roll(odd_part, 1, axis=-1)  21.6 us
    reduce_scatter x1, waiting for transfers between devices, on_device(): lax.psum_scatter(increment, 'mem', scatter_dimension=1, tiled=True)  20 us
    another operation x3, local copies, waits for them, and re-layouts, widen_lon(): jnp.stack([coarse, odd_part], axis=-1)  18.6 us
  transfers between devices with their start and end apart: 13, of which 7 were waited for; matrix products, arithmetic and copies ran while one was open for 2% of the time, Pallas kernels for 0%

profile of v1, /device:TPU:0, one launch (start us, length us, event | category | flops | bytes accessed | tf_op | source)
XLA Modules:
  0.0 610.1 jit_solution(13759581346806380157)
XLA Ops:
  9.4 11.3 %scatter_custom_fusion = f32[32768]{0:T(1024)S(1)} fusion(s32[2048]{0:T(1024)S(1)} %bitcast.168, f32[2048]{0:T(1024)S(1)} %multiply_select_fusion.2, f32[]{:T(128)} %constant.31.clone.1), kind=kCustom, calls=%fused_computation.133 | custom fusion | flops 2048 | bytes 131076 | tf_op jit(solution)/shard_map/scatter-add | solution.py:104
  24.5 4.3 reduce_sum.135
  28.8 4.8 copy.34
  33.6 7.2 %fusion.188 = (f32[16,8,1024,1]{0,1,3,2:T(8,128)}, f32[16,8,1024,1]{0,1,3,2:T(8,128)}) fusion(f32[16,8,1024,2]{0,1,3,2:T(8,128)} %bitcast.146), kind=kLoop, calls=%fused_computation.221 | loop fusion | bytes 2097152 | tf_op jit(solution)/shard_map/slice | solution.py:62
  46.9 4.0 fusion.14
  50.9 4.9 collective-permute-start
  58.1 10.6 %select_add_fusion = f32[8,24]{1,0:T(8,128)S(1)} fusion(f32[]{:T(128)} %bitcast.25, f32[]{:T(128)} %bitcast.24, f32[]{:T(128)} %bitcast.23, f32[]{:T(128)} %bitcast.22, f32[]{:T(128)} %bitcast.21, f32[]{:T(128)} %bitcast.20, f32[]{:T(128)} %bitcast.19, f32[]{:T(128)} %bitcast.18, f32[]{:T(128)} %bitcast.17, f32[]{:T(128)} %bitcast.16, f32[]{:T(128)} %bitcast.15, ...), kind=kLoop, calls=%fused_computation.169 | loop fusion | flops 9792 | bytes 836 | tf_op jit(solution)/shard_map/add | solution.py:48
  68.7 9.5 %collective-permute-done = f32[16,8,1024]{2,1,0:T(8,128)S(1)} collective-permute-done((f32[16,8,1024]{2,1,0:T(8,128)S(1)}, f32[16,8,1024]{2,1,0:T(8,128)S(1)}, u32[]{:S(2)}, u32[]{:S(2)}) %collective-permute-start) | collective-permute-done | bytes 524320 | tf_op jit(solution)/shard_map/ppermute | solution.py:21
  79.9 4.4 collective-permute-start.2
  85.6 20.2 %collective-permute-done.2 = f32[16,8,1024]{2,1,0:T(8,128)S(1)} collective-permute-done((f32[16,8,1024]{2,1,0:T(8,128)S(1)}, f32[16,8,1024]{2,1,0:T(8,128)S(1)}, u32[]{:S(2)}, u32[]{:S(2)}) %collective-permute-start.2) | collective-permute-done | bytes 524320 | tf_op jit(solution)/shard_map/ppermute | solution.py:21
  106.7 3.9 fusion.12
  111.1 6.2 %copy.37 = f32[16,8,1024,2]{0,1,3,2:T(8,128)} copy(f32[16,8,1024,2]{2,1,0,3:T(8,128)S(1)} %pad_maximum_fusion) | data formatting | bytes 2097152 | tf_op jit(solution)/shard_map/stack | solution.py:54
  117.3 5.4 copy.38
  125.2 3.7 reshape.188
  130.8 16.6 %gather_fusion = f32[2048]{0:T(1024)S(1)} fusion(f32[16,2048]{1,0:T(8,128)S(1)} %broadcast_multiply_fusion.2, s32[2048]{0:T(1024)S(1)} %bitcast.140), kind=kCustom, calls=%fused_computation | custom fusion | bytes 32768 | tf_op jit(solution)/shard_map/gather | solution.py:128
  147.4 5.2 all-gather
  153.3 43.9 %all-reduce.2 = (f32[]{:T(128)}, f32[]{:T(128)}) all-reduce(f32[]{:T(128)} %get-tuple-element.20, f32[]{:T(128)} %fusion.124), channel_id=1, replica_groups=mesh['mem'=4,'lat'=8] {'mem','lat'}, use_global_device_ids=true, to_apply=%region_3.4 | all-reduce | flops 2 | bytes 16 | tf_op jit(solution)/shard_map/psum | solution.py:118
  199.2 11.3 %scatter_custom_fusion.1 = f32[32768]{0:T(1024)S(1)} fusion(s32[2048]{0:T(1024)S(1)} %bitcast.169, f32[2048]{0:T(1024)S(1)} %multiply_select_fusion.1, f32[]{:T(128)} %constant.31.clone.1), kind=kCustom, calls=%fused_computation.131 | custom fusion | flops 2048 | bytes 131076 | tf_op jit(solution)/shard_map/scatter-add | solution.py:104
  215.6 4.3 reduce_sum.140
  219.9 4.8 copy.39
  224.7 7.2 %fusion.187 = (f32[16,8,1024,1]{0,1,3,2:T(8,128)}, f32[16,8,1024,1]{0,1,3,2:T(8,128)}) fusion(f32[16,8,1024,2]{0,1,3,2:T(8,128)} %bitcast.147), kind=kLoop, calls=%fused_computation.220 | loop fusion | bytes 2097152 | tf_op jit(solution)/shard_map/slice | solution.py:62
  237.9 4.0 fusion.10
  241.9 4.5 collective-permute-start.4
  247.9 20.1 %collective-permute-done.4 = f32[16,8,1024]{2,1,0:T(8,128)S(1)} collective-permute-done((f32[16,8,1024]{2,1,0:T(8,128)S(1)}, f32[16,8,1024]{2,1,0:T(8,128)S(1)}, u32[]{:S(2)}, u32[]{:S(2)}) %collective-permute-start.4) | collective-permute-done | bytes 524320 | tf_op jit(solution)/shard_map/ppermute | solution.py:21
  269.6 4.4 collective-permute-start.6
  275.4 19.4 %collective-permute-done.6 = f32[16,8,1024]{2,1,0:T(8,128)S(1)} collective-permute-done((f32[16,8,1024]{2,1,0:T(8,128)S(1)}, f32[16,8,1024]{2,1,0:T(8,128)S(1)}, u32[]{:S(2)}, u32[]{:S(2)}) %collective-permute-start.6) | collective-permute-done | bytes 524320 | tf_op jit(solution)/shard_map/ppermute | solution.py:21
  295.7 3.9 fusion.8
  300.1 6.2 %copy.42 = f32[16,8,1024,2]{0,1,3,2:T(8,128)} copy(f32[16,8,1024,2]{2,1,0,3:T(8,128)S(1)} %pad_maximum_fusion.1) | data formatting | bytes 2097152 | tf_op jit(solution)/shard_map/stack | solution.py:54
  306.3 5.4 copy.43
  319.8 16.6 %gather_fusion.1 = f32[2048]{0:T(1024)S(1)} fusion(f32[16,2048]{1,0:T(8,128)S(1)} %broadcast_multiply_fusion.1, s32[2048]{0:T(1024)S(1)} %bitcast.141), kind=kCustom, calls=%fused_computation.1 | custom fusion | bytes 32768 | tf_op jit(solution)/shard_map/gather | solution.py:128
  336.4 5.2 all-gather.1
  342.3 44.0 %all-reduce.1 = (f32[]{:T(128)}, f32[]{:T(128)}) all-reduce(f32[]{:T(128)} %get-tuple-element.18, f32[]{:T(128)} %fusion.125), channel_id=1, replica_groups=mesh['mem'=4,'lat'=8] {'mem','lat'}, use_global_device_ids=true, to_apply=%region_11.12 | all-reduce | flops 2 | bytes 16 | tf_op jit(solution)/shard_map/psum | solution.py:118
  389.0 11.4 %scatter_custom_fusion.2 = f32[32768]{0:T(1024)S(1)} fusion(s32[2048]{0:T(1024)} %bitcast.170, f32[2048]{0:T(1024)S(1)} %get-tuple-element.8, f32[]{:T(128)} %constant.31.clone.1), kind=kCustom, calls=%fused_computation.129 | custom fusion | flops 2048 | bytes 131584 | tf_op jit(solution)/shard_map/scatter-add | solution.py:104
  405.5 4.3 reduce_sum.145
  409.8 4.8 copy.44
  414.6 7.2 %fusion.186 = (f32[16,8,1024,1]{0,1,3,2:T(8,128)}, f32[16,8,1024,1]{0,1,3,2:T(8,128)}) fusion(f32[16,8,1024,2]{0,1,3,2:T(8,128)} %bitcast.148), kind=kLoop, calls=%fused_computation.219 | loop fusion | bytes 2097152 | tf_op jit(solution)/shard_map/slice | solution.py:62
  428.5 5.1 fusion.6
  433.5 4.5 collective-permute-start.8
  439.6 20.2 %collective-permute-done.8 = f32[16,8,1024]{2,1,0:T(8,128)S(1)} collective-permute-done((f32[16,8,1024]{2,1,0:T(8,128)S(1)}, f32[16,8,1024]{2,1,0:T(8,128)S(1)}, u32[]{:S(2)}, u32[]{:S(2)}) %collective-permute-start.8) | collective-permute-done | bytes 524320 | tf_op jit(solution)/shard_map/ppermute | solution.py:21
  462.2 4.4 collective-permute-start.10
  467.9 19.6 %collective-permute-done.10 = f32[16,8,1024]{2,1,0:T(8,128)S(1)} collective-permute-done((f32[16,8,1024]{2,1,0:T(8,128)S(1)}, f32[16,8,1024]{2,1,0:T(8,128)S(1)}, u32[]{:S(2)}, u32[]{:S(2)}) %collective-permute-start.10) | collective-permute-done | bytes 524320 | tf_op jit(solution)/shard_map/ppermute | solution.py:21
  489.6 3.9 fusion.4
  494.0 6.2 %copy.47 = f32[16,8,1024,2]{0,1,3,2:T(8,128)} copy(f32[16,8,1024,2]{2,1,0,3:T(8,128)S(1)} %pad_maximum_fusion.2) | data formatting | bytes 2097152 | tf_op jit(solution)/shard_map/stack | solution.py:54
  500.2 5.4 copy.48
  513.7 16.6 %gather_fusion.2 = f32[2048]{0:T(1024)S(1)} fusion(f32[16,2048]{1,0:T(8,128)S(1)} %broadcast_multiply_fusion, s32[2048]{0:T(1024)S(1)} %bitcast.142), kind=kCustom, calls=%fused_computation.2 | custom fusion | bytes 32768 | tf_op jit(solution)/shard_map/gather | solution.py:128
  530.3 5.2 all-gather.2
  536.3 42.8 %all-reduce = (f32[]{:T(128)}, f32[]{:T(128)}) all-reduce(f32[]{:T(128)} %get-tuple-element.17, f32[]{:T(128)} %fusion.126), channel_id=1, replica_groups=mesh['mem'=4,'lat'=8] {'mem','lat'}, use_global_device_ids=true, to_apply=%region_19.20 | all-reduce | flops 2 | bytes 16 | tf_op jit(solution)/shard_map/psum | solution.py:118
  582.8 20.0 %reduce-scatter.2.cloned.1.call-done = f32[16,512]{1,0:T(8,128)} async-done(((f32[16,2048]{1,0:T(8,128)}), f32[16,512]{1,0:T(8,128)}) %reduce-scatter.2.cloned.1.call-update) | async-done | bytes 32784 | tf_op jit(solution)/shard_map/reduce_scatter | solution.py:135
  (101 shorter events, 79.0 us)
Async XLA Ops:
  7.2 595.6 %reduce-scatter.2.cloned.1.call-start = ((), (), s32[]{:S(2)}) async-start(), calls=%async_computation.1 | async-start | bytes 163840 | tf_op jit(solution)/shard_map/reduce_scatter | solution.py:135
  8.7 190.5 %copy-start.10 = (s32[2048,1]{0,1:T(1,128)}, s32[2048,1]{0,1:T(1,128)S(1)}, u32[]{:S(2)}) copy-start(s32[2048,1]{0,1:T(1,128)S(1)} %get-tuple-element.23) | copy-start | bytes 24580
  50.9 27.3 %collective-permute-start = (f32[16,8,1024]{2,1,0:T(8,128)S(1)}, f32[16,8,1024]{2,1,0:T(8,128)S(1)}, u32[]{:S(2)}, u32[]{:S(2)}) collective-permute-start(f32[16,8,1024]{2,1,0:T(8,128)S(1)} %fusion.14), channel_id=1, source_target_pairs={{0,1},{1,2},{2,3},{3,4},{4,5},{5,6},{6,7},{8,9},{9,10},{10,11},{11... | collective-permute-start | bytes 1572872 | tf_op jit(solution)/shard_map/ppermute | solution.py:21
  55.8 22.4 %collective-permute-start.1 = (f32[16,8,1024]{2,1,0:T(8,128)S(1)}, f32[16,8,1024]{2,1,0:T(8,128)S(1)}, u32[]{:S(2)}, u32[]{:S(2)}) collective-permute-start(f32[16,8,1024]{2,1,0:T(8,128)S(1)} %fusion.14), channel_id=1, source_target_pairs={{1,0},{2,1},{3,2},{4,3},{5,4},{6,5},{7,6},{9,8},{10,9},{11,10},{12... | collective-permute-start | bytes 1572872 | tf_op jit(solution)/shard_map/ppermute | solution.py:24
  68.7 226.1 %copy-start.7 = (f32[8,24]{1,0:T(8,128)}, f32[8,24]{1,0:T(8,128)S(1)}, u32[]{:S(2)}) copy-start(f32[8,24]{1,0:T(8,128)S(1)} %select_add_fusion) | copy-start | bytes 2308
  79.9 25.9 %collective-permute-start.2 = (f32[16,8,1024]{2,1,0:T(8,128)S(1)}, f32[16,8,1024]{2,1,0:T(8,128)S(1)}, u32[]{:S(2)}, u32[]{:S(2)}) collective-permute-start(f32[16,8,1024]{2,1,0:T(8,128)S(1)} %get-tuple-element.21), channel_id=1, source_target_pairs={{0,1},{1,2},{2,3},{3,4},{4,5},{5,6},{6,7},{8,9},{9,10},{10,11},{11... | collective-permute-start | bytes 1572872 | tf_op jit(solution)/shard_map/ppermute | solution.py:21
  84.3 21.5 %collective-permute-start.3 = (f32[16,8,1024]{2,1,0:T(8,128)S(1)}, f32[16,8,1024]{2,1,0:T(8,128)S(1)}, u32[]{:S(2)}, u32[]{:S(2)}) collective-permute-start(f32[16,8,1024]{2,1,0:T(8,128)S(1)} %get-tuple-element.21), channel_id=1, source_target_pairs={{1,0},{2,1},{3,2},{4,3},{5,4},{6,5},{7,6},{9,8},{10,9},{11,10},{12... | collective-permute-start | bytes 1572872 | tf_op jit(solution)/shard_map/ppermute | solution.py:24
  122.7 6.2 %copy-start = (bf16[16,16,2048]{2,1,0:T(8,128)(2,1)S(1)}, bf16[16,16,2048]{2,1,0:T(8,128)(2,1)}, u32[]{:S(2)}) copy-start(bf16[16,16,2048]{2,1,0:T(8,128)(2,1)} %param.5) | copy-start | bytes 3145732
  130.7 21.9 %copy-start.2 = (f32[1,2048]{1,0:T(1,128)S(1)}, f32[1,2048]{1,0:T(1,128)}, u32[]{:S(2)}) copy-start(f32[1,2048]{1,0:T(1,128)} %param.9) | copy-start | bytes 24580
  130.8 21.9 %copy-start.3 = (f32[1,2048]{1,0:T(1,128)S(1)}, f32[1,2048]{1,0:T(1,128)}, u32[]{:S(2)}) copy-start(f32[1,2048]{1,0:T(1,128)} %param.8) | copy-start | bytes 24580
  152.7 67.2 %copy-start.5 = (f32[2048]{0:T(1024)}, f32[2048]{0:T(1024)S(1)}, u32[]{:S(2)}) copy-start(f32[2048]{0:T(1024)S(1)} %reduce_sum.138) | copy-start | bytes 24580
  241.9 26.1 %collective-permute-start.4 = (f32[16,8,1024]{2,1,0:T(8,128)S(1)}, f32[16,8,1024]{2,1,0:T(8,128)S(1)}, u32[]{:S(2)}, u32[]{:S(2)}) collective-permute-start(f32[16,8,1024]{2,1,0:T(8,128)S(1)} %fusion.10), channel_id=1, source_target_pairs={{0,1},{1,2},{2,3},{3,4},{4,5},{5,6},{6,7},{8,9},{9,10},{10,11},{11... | collective-permute-start | bytes 1572872 | tf_op jit(solution)/shard_map/ppermute | solution.py:21
  246.4 21.6 %collective-permute-start.5 = (f32[16,8,1024]{2,1,0:T(8,128)S(1)}, f32[16,8,1024]{2,1,0:T(8,128)S(1)}, u32[]{:S(2)}, u32[]{:S(2)}) collective-permute-start(f32[16,8,1024]{2,1,0:T(8,128)S(1)} %fusion.10), channel_id=1, source_target_pairs={{1,0},{2,1},{3,2},{4,3},{5,4},{6,5},{7,6},{9,8},{10,9},{11,10},{12... | collective-permute-start | bytes 1572872 | tf_op jit(solution)/shard_map/ppermute | solution.py:24
  269.6 25.2 %collective-permute-start.6 = (f32[16,8,1024]{2,1,0:T(8,128)S(1)}, f32[16,8,1024]{2,1,0:T(8,128)S(1)}, u32[]{:S(2)}, u32[]{:S(2)}) collective-permute-start(f32[16,8,1024]{2,1,0:T(8,128)S(1)} %get-tuple-element.19), channel_id=1, source_target_pairs={{0,1},{1,2},{2,3},{3,4},{4,5},{5,6},{6,7},{8,9},{9,10},{10,11},{11... | collective-permute-start | bytes 1572872 | tf_op jit(solution)/shard_map/ppermute | solution.py:21
  274.1 20.7 %collective-permute-start.7 = (f32[16,8,1024]{2,1,0:T(8,128)S(1)}, f32[16,8,1024]{2,1,0:T(8,128)S(1)}, u32[]{:S(2)}, u32[]{:S(2)}) collective-permute-start(f32[16,8,1024]{2,1,0:T(8,128)S(1)} %get-tuple-element.19), channel_id=1, source_target_pairs={{1,0},{2,1},{3,2},{4,3},{5,4},{6,5},{7,6},{9,8},{10,9},{11,10},{12... | collective-permute-start | bytes 1572872 | tf_op jit(solution)/shard_map/ppermute | solution.py:24
  319.7 21.9 %copy-start.4 = (f32[1,2048]{1,0:T(1,128)S(1)}, f32[1,2048]{1,0:T(1,128)}, u32[]{:S(2)}) copy-start(f32[1,2048]{1,0:T(1,128)} %param.8) | copy-start | bytes 24580
  319.7 21.9 %copy-start.6 = (f32[2048]{0:T(1024)S(1)}, f32[2048]{0:T(1024)}, u32[]{:S(2)}) copy-start(f32[2048]{0:T(1024)} %copy-done.5) | copy-start | bytes 24580
  428.5 31.3 %copy-start.8 = (f32[8,24]{1,0:T(8,128)S(1)}, f32[8,24]{1,0:T(8,128)}, u32[]{:S(2)}) copy-start(f32[8,24]{1,0:T(8,128)} %copy-done.7) | copy-start | bytes 2308
  433.5 26.3 %collective-permute-start.8 = (f32[16,8,1024]{2,1,0:T(8,128)S(1)}, f32[16,8,1024]{2,1,0:T(8,128)S(1)}, u32[]{:S(2)}, u32[]{:S(2)}) collective-permute-start(f32[16,8,1024]{2,1,0:T(8,128)S(1)} %fusion.6), channel_id=1, source_target_pairs={{0,1},{1,2},{2,3},{3,4},{4,5},{5,6},{6,7},{8,9},{9,10},{10,11},{11... | collective-permute-start | bytes 1572872 | tf_op jit(solution)/shard_map/ppermute | solution.py:21
  438.0 21.8 %collective-permute-start.9 = (f32[16,8,1024]{2,1,0:T(8,128)S(1)}, f32[16,8,1024]{2,1,0:T(8,128)S(1)}, u32[]{:S(2)}, u32[]{:S(2)}) collective-permute-start(f32[16,8,1024]{2,1,0:T(8,128)S(1)} %fusion.6), channel_id=1, source_target_pairs={{1,0},{2,1},{3,2},{4,3},{5,4},{6,5},{7,6},{9,8},{10,9},{11,10},{12... | collective-permute-start | bytes 1572872 | tf_op jit(solution)/shard_map/ppermute | solution.py:24
  462.2 25.3 %collective-permute-start.10 = (f32[16,8,1024]{2,1,0:T(8,128)S(1)}, f32[16,8,1024]{2,1,0:T(8,128)S(1)}, u32[]{:S(2)}, u32[]{:S(2)}) collective-permute-start(f32[16,8,1024]{2,1,0:T(8,128)S(1)} %get-tuple-element.16), channel_id=1, source_target_pairs={{0,1},{1,2},{2,3},{3,4},{4,5},{5,6},{6,7},{8,9},{9,10},{10,11},{11... | collective-permute-start | bytes 1572872 | tf_op jit(solution)/shard_map/ppermute | solution.py:21
  466.6 20.9 %collective-permute-start.11 = (f32[16,8,1024]{2,1,0:T(8,128)S(1)}, f32[16,8,1024]{2,1,0:T(8,128)}, u32[]{:S(2)}, u32[]{:S(2)}) collective-permute-start(f32[16,8,1024]{2,1,0:T(8,128)S(1)} %get-tuple-element.16), channel_id=1, source_target_pairs={{1,0},{2,1},{3,2},{4,3},{5,4},{6,5},{7,6},{9,8},{10,9},{11,10},{12... | collective-permute-start | bytes 1572872 | tf_op jit(solution)/shard_map/ppermute | solution.py:24
  513.7 21.9 %copy-start.9 = (f32[2048]{0:T(1024)S(1)}, f32[2048]{0:T(1024)}, u32[]{:S(2)}) copy-start(f32[2048]{0:T(1024)} %get-tuple-element.9) | copy-start | bytes 24580
  513.7 68.1 %copy-start.1 = (f32[16,8,1024]{2,1,0:T(8,128)S(1)}, f32[16,8,1024]{2,1,0:T(8,128)}, u32[]{:S(2)}) copy-start(f32[16,8,1024]{2,1,0:T(8,128)} %get-tuple-element.42) | copy-start | bytes 1572868
Sparse Core Ops, SparseCore 0:
  581.9 20.8 reduce-scatter.1
